TPU v7x, 128 devices: a whole 4x4x4 slice. The times are simulated.
128 devices in a mesh: left: 32 (over z, y_lo, x), right: 4 (over y_hi, core).
Axes of the slice: x: 4, y: 4 (y_hi: 2, y_lo: 2; y = y_hi * 2 + y_lo), z: 4, core: 2. Of those that a mesh axis runs over, the one named last changes fastest.
Arguments:
- density: float32 [512, 512, 2048], P(None, 'left', 'right'), may hold values from -6 to 6
- symbol_x: float32 [512], replicated, may hold values from 0.3 to 3
- symbol_y: float32 [512], replicated, may hold values from 0.3 to 3
- symbol_z: float32 [2048], replicated, may hold values from 0.3 to 3
Outputs:
- spectrum: float32 [512, 512, 2048], P('left', 'right')
All inputs are finite; a program needn't handle non-finite values.
Results may differ from a plain program's by a relative error of at most 0.00007.
Values sent between devices are 32-bit elements; how exact they have to be, the bound alone decides.
No kernel may reach another device: no remote copies, remote signals or barrier semaphores. Data moves between devices by JAX's collectives and lax.ppermute only.
A program may use at most 192 MiB of HBM per device.

v0:
```python
import functools

import jax
import jax.numpy as jnp
import numpy as np
from jax import lax
from jax.experimental import pallas as pl
from jax.experimental.pallas import tpu as pltpu
from jax.sharding import PartitionSpec as P

CUTS = (0, 2, 7, 11, 14, 16)
F32 = jnp.float32
BF16 = jnp.bfloat16


def turns(rows, cols, count):
    return 2.0 * np.pi / count * (np.asarray(rows)[:, None] * np.asarray(cols)[None, :] % count)


def mode_rows(rows, cols, count):
    angle = turns(rows, cols, count)
    return ((np.cos(angle) + np.sin(angle)) * count**-0.5).astype(np.float32)


def np_halves(table):
    high = table.astype(jnp.bfloat16)
    low = (table - high.astype(np.float32)).astype(jnp.bfloat16)
    return jnp.asarray(high), jnp.asarray(low)


def halves(value):
    high = value.astype(BF16)
    return high, (value - high.astype(F32)).astype(BF16)


def dot(a, b):
    return jnp.dot(a, b, preferred_element_type=F32)


def x_kernel(values, tables, out):
    count, rows, lanes = values.shape
    half = count // 2
    flat = values.reshape(count * rows, lanes)
    z = pl.ds(pl.multiple_of(pl.program_id(1) * lanes, lanes), lanes)
    results = {}
    for row in range(0, rows, 2):
        first = [flat[pl.ds(row + k, half, stride=rows), :] for k in range(2)]
        second = [flat[pl.ds(half * rows + row + k, half, stride=rows), :] for k in range(2)]
        first = jnp.concatenate(first, axis=1)
        second = jnp.concatenate(second, axis=1)
        for parity, mixed, high, low in (
            (0, first + second, tables[0], tables[1]),
            (1, first - second, tables[2], tables[3]),
        ):
            mixed_high, mixed_low = halves(mixed)
            both = dot(jnp.concatenate([high, low], axis=0), mixed_high)
            done = both[:half] + both[half:] + dot(high, mixed_low)
            for k in range(2):
                results[parity, row + k] = done[:, k * lanes : (k + 1) * lanes]
    for parity in range(2):
        stack = jnp.stack([results[parity, row] for row in range(rows)], axis=0)
        out.reshape(half, 2, *out.shape[1:])[:, parity, pl.ds(pl.multiple_of(pl.program_id(0) * rows, rows), rows), z] = jnp.swapaxes(stack, 0, 1)


def fold_tables(count):
    first = np.arange(count // 2)
    even = mode_rows(np.arange(0, count, 2), first, count)
    odd = mode_rows(np.arange(1, count, 2), first, count)
    return jnp.stack(np_halves(even) + np_halves(odd))


def x_modes(density):
    nx, ny, nz = density.shape
    half = nx // 2
    rows, lanes = 8, 128
    block = pl.BlockSpec((nx, rows, lanes), lambda i, k: (0, i, k))
    return pl.pallas_call(
        x_kernel,
        grid=(ny // rows, nz // lanes),
        in_specs=[block, pl.BlockSpec((4, half, half), lambda i, k: (0, 0, 0))],
        out_specs=pl.BlockSpec(memory_space=pltpu.VMEM),
        out_shape=pltpu.VMEM((nx, ny, nz), F32),
        compiler_params=pltpu.CompilerParams(vmem_limit_bytes=43 * 2**20),
        name="x_modes",
    )(density, fold_tables(nx))


def y_kernel(own, values, *rest, right):
    tables, outs = rest[: 2 * right], rest[2 * right :]
    parts, _, part, nz = values.shape
    share = outs[0].shape[1]
    high = jnp.concatenate([table[...] for table in tables[:right]], axis=0)
    low = jnp.concatenate([table[...] for table in tables[right:]], axis=0)
    full_high, full_low = halves(values[...].reshape(parts * part, nz))
    done = dot(high, full_high) + dot(low, full_high) + dot(high, full_low)
    for k, out in enumerate(outs):
        out[0] = done[k * share : (k + 1) * share]


def y_modes(values, own, lo, hi, right):
    parts, _, part, nz = values.shape
    ny = parts * part
    share = ny // right
    tables = np_halves(mode_rows(np.arange(ny), np.arange(ny), ny))
    pick = [pl.BlockSpec((share, ny), lambda j, own, k=k: (own[0] ^ k, 0)) for k in range(right)]
    return pl.pallas_call(
        functools.partial(y_kernel, right=right),
        grid_spec=pltpu.PrefetchScalarGridSpec(
            num_scalar_prefetch=1,
            grid=(hi - lo,),
            in_specs=[pl.BlockSpec((parts, 1, part, nz), lambda j, own: (0, lo + j, 0, 0))] + pick * 2,
            out_specs=[pl.BlockSpec((1, share, nz), lambda j, own: (j, 0, 0))] * right,
        ),
        out_shape=[jax.ShapeDtypeStruct((hi - lo, share, nz), F32)] * right,
        name="y_modes",
    )(own, values, *[table for table in tables for _ in range(right)])


def z_kernel(part_x, high, low, part_y, symbol_z, *rest, lo, count, summed, last):
    values = rest[:count]
    out, mine = rest[-2:]
    own, share, width = values[0].shape
    rows = own * share

    @pl.when(pl.program_id(0) == 0)
    def _():
        for r in range(count):
            value_high, value_low = halves(values[r][...].reshape(rows, width))
            mine[:rows, r * width : (r + 1) * width] = value_high
            mine[rows:, r * width : (r + 1) * width] = value_low

    both = dot(mine[...], high[...])
    done = both[:rows] + both[rows:] + dot(mine[:rows], low[...])
    for j in range(own):
        result = done[j * share : (j + 1) * share]
        if summed:
            result = result + rest[count][j]
        if last:
            result = result * lax.rsqrt(part_x[lo + j] + part_y[...] + symbol_z[...])
        out[j] = result


def z_modes(values, places, tables, symbols, lo, sums=None, out=None, last=True):
    count = len(values)
    own, share, width = values[0].shape
    part_x, part_y, symbol_z = symbols
    nz = symbol_z.shape[1]
    lanes = 256 if count > 1 else 512
    cols = pl.BlockSpec((count * width, lanes), lambda n: (places[0] // count, n))
    sum_block = pl.BlockSpec((own, share, lanes), lambda n: (0, 0, n))
    in_specs = [
        pl.BlockSpec(memory_space=pltpu.SMEM),
        cols,
        cols,
        pl.BlockSpec((share, 1), lambda n: (0, 0)),
        pl.BlockSpec((1, lanes), lambda n: (0, n)),
    ] + [pl.BlockSpec((own, share, width), lambda n: (0, 0, 0))] * count
    args = [part_x, *tables, part_y, symbol_z, *values]
    if sums is not None:
        in_specs.append(sum_block)
        args.append(sums)
    aliases = {}
    if out is not None:
        aliases = {len(args): 0}
        in_specs.append(pl.BlockSpec(memory_space=pl.ANY))
        args.append(out)
    full_block = pl.BlockSpec((pl.Element(own), pl.Element(share), pl.Element(lanes)), lambda n: (lo, 0, n * lanes))
    return pl.pallas_call(
        functools.partial(z_kernel, lo=lo, count=count, summed=sums is not None, last=last),
        grid=(nz // lanes,),
        in_specs=in_specs,
        out_specs=full_block if last else sum_block,
        out_shape=jax.ShapeDtypeStruct((part_x.shape[0] if last else own, share, nz), F32),
        scratch_shapes=[pltpu.VMEM((2 * own * share, count * width), BF16)],
        input_output_aliases=aliases,
        name="z_modes",
    )(*args)


def run_halves(table):
    high = lax.reduce_precision(table, 8, 7)
    return high.astype(BF16), (table - high).astype(BF16)


def angles(rows, cols, count):
    return 2.0 * jnp.pi / count * (rows[:, None] * cols[None, :] % count).astype(F32)


def z_tables(nz, right, own, zero):
    step = 64
    share = nz // right
    cols = jnp.arange(nz) + zero
    rank = jnp.arange(0, nz, step) + zero
    coarse = angles(((rank // share) ^ own) * share + rank % share, cols, nz)
    fine = angles(jnp.arange(step), cols, nz)
    cos, sin = jnp.cos(fine) * nz**-0.5, jnp.sin(fine) * nz**-0.5
    near, back, cos, sin = lax.optimization_barrier((cos + sin, cos - sin, jnp.cos(coarse), jnp.sin(coarse)))
    high, low = run_halves(cos[:, None, :] * near[None] + sin[:, None, :] * back[None])
    return high.reshape(nz, nz), low.reshape(nz, nz)


def per_device(density, symbol_x, symbol_y, symbol_z):
    left = lax.axis_size("left")
    right = lax.axis_size("right")
    nx, ny_part, nz_part = density.shape
    share_x = nx // left
    share_y = ny_part * left // right
    a = x_modes(density).reshape(left, share_x, ny_part, nz_part)
    at_left = lax.axis_index("left").astype(jnp.int32)
    at_right = lax.axis_index("right").astype(jnp.int32)[None]
    a, at_left, at_right = lax.optimization_barrier((a, at_left, at_right))
    a = lax.all_to_all(a, "left", split_axis=0, concat_axis=0, tiled=True)
    sent = []
    for c, (lo, hi) in enumerate(zip(CUTS, CUTS[1:])):
        b = y_modes(a, at_right, lo, hi, right)
        a, mine, at_left, zero = lax.optimization_barrier((a, b[0], at_left, jnp.int32(0)))
        met = [mine]
        for k in range(1, right):
            met.append(lax.ppermute(b[k], "right", [(r, r ^ k) for r in range(right)]))
        sent.append(met)
        if c == 1:
            at = at_right[0] + zero
            tables = z_tables(nz_part * right, right, at, zero)
            part_x = lax.dynamic_slice_in_dim(symbol_x, at_left * share_x, share_x)
            part_y = lax.dynamic_slice_in_dim(symbol_y, at * share_y, share_y)[:, None]
            symbols = (part_x, part_y, symbol_z[None])
    out = None
    for c, (lo, hi) in enumerate(zip(CUTS, CUTS[1:])):
        met = sent[c]
        if hi < share_x:
            out = z_modes(met, range(right), tables, symbols, lo, out=out)
        else:
            half = right // 2
            sums = z_modes(met[:half], range(half), tables, symbols, lo, last=False)
            for k in range(half, right - 1):
                sums, out = lax.optimization_barrier((sums, out))
                sums = z_modes(met[k : k + 1], (k,), tables, symbols, lo, sums=sums, last=False)
            out = z_modes(met[-1:], (right - 1,), tables, symbols, lo, sums=sums, out=out)
    return out


def solution(mesh):
    return jax.shard_map(
        per_device,
        mesh=mesh,
        in_specs=(P(None, "left", "right"), P(), P(), P()),
        out_specs=P("left", "right", None),
        check_vma=False,
    )
```

profile of v0, /device:TPU:1, one launch (start us, length us, event | category | flops | bytes accessed | tf_op | source)
XLA Modules:
  0.0 474.6 jit_solution(12379401542172731078)
XLA Ops:
  0.0 14.3 %x_modes.1 = f32[512,16,512]{2,1,0:T(8,128)S(1)} custom-call(f32[512,16,512]{2,1,0:T(8,128)} %values.1, bf16[4,256,256]{2,1,0:T(8,128)(2,1)} %constant.95.tables), custom_call_target="tpu_custom_call" | custom-call | tf_op jit(solution)/shard_map/x_modes/pallas_call | solution.py:77
  14.3 193.6 %all_to_all.5.values = f32[32,16,16,512]{3,2,1,0:T(8,128)} all-to-all(f32[32,16,16,512]{3,2,1,0:T(8,128)S(1)} %bitcast.9), channel_id=1, replica_groups=mesh['left'=32,'right'=4] {'left'}, dimensions={0} | all-to-all | bytes 33554432 | tf_op jit(solution)/shard_map/all_to_all | solution.py:212
  207.9 4.4 y_modes.5
  212.4 8.6 %y_modes.6 = (f32[5,128,512]{2,1,0:T(8,128)}, f32[5,128,512]{2,1,0:T(8,128)}, f32[5,128,512]{2,1,0:T(8,128)}, f32[5,128,512]{2,1,0:T(8,128)}) custom-call(s32[1]{0:T(128)} %bitcast.1.own, f32[32,16,16,512]{3,2,1,0:T(8,128)} %all_to_all.5.values, bf16[512,512]{1,0:T(8,128)(2,1)} %constant.88.clone.rest_0_.rest_1_.rest_2_.rest_3_, ...), custom_call_target="tpu_custom_call" | custom-call | tf_op jit(solution)/shard_map/y_modes/pallas_call | solution.py:106
  221.0 7.0 %y_modes.7 = (f32[4,128,512]{2,1,0:T(8,128)}, f32[4,128,512]{2,1,0:T(8,128)}, f32[4,128,512]{2,1,0:T(8,128)}, f32[4,128,512]{2,1,0:T(8,128)}) custom-call(s32[1]{0:T(128)} %bitcast.1.own, f32[32,16,16,512]{3,2,1,0:T(8,128)} %all_to_all.5.values, bf16[512,512]{1,0:T(8,128)(2,1)} %constant.88.clone.rest_0_.rest_1_.rest_2_.rest_3_, ...), custom_call_target="tpu_custom_call" | custom-call | tf_op jit(solution)/shard_map/y_modes/pallas_call | solution.py:106
  228.0 2.2 collective-permute-start.6
  230.2 0.1 collective-permute-start.12
  230.3 2.6 collective-permute-start.13
  232.9 0.9 collective-permute-start.14
  233.8 5.9 %y_modes.8 = (f32[3,128,512]{2,1,0:T(8,128)}, f32[3,128,512]{2,1,0:T(8,128)}, f32[3,128,512]{2,1,0:T(8,128)}, f32[3,128,512]{2,1,0:T(8,128)}) custom-call(s32[1]{0:T(128)} %bitcast.1.own, f32[32,16,16,512]{3,2,1,0:T(8,128)} %all_to_all.5.values, bf16[512,512]{1,0:T(8,128)(2,1)} %constant.88.clone.rest_0_.rest_1_.rest_2_.rest_3_, ...), custom_call_target="tpu_custom_call" | custom-call | tf_op jit(solution)/shard_map/y_modes/pallas_call | solution.py:106
  239.7 4.5 y_modes.9
  244.2 0.0 collective-permute-start.2
  244.2 2.1 fusion.7
  246.4 0.8 copy-done.7
  247.2 0.5 collective-permute-start.9
  247.7 0.0 collective-permute-done.13.rest_2_
  247.7 0.8 copy-done.8
  248.5 2.6 collective-permute-start.10
  251.1 6.5 %collective-permute-done.14.rest_3_ = f32[2,128,512]{2,1,0:T(8,128)S(1)} collective-permute-done((f32[2,128,512]{2,1,0:T(8,128)}, f32[2,128,512]{2,1,0:T(8,128)S(1)}, u32[]{:S(2)}, u32[]{:S(2)}) %collective-permute-start.14) | collective-permute-done | bytes 524320 | tf_op jit(solution)/shard_map/ppermute | solution.py:219
  257.6 1.4 collective-permute-start.11
  259.0 0.0 collective-permute-done.2.rest_1_
  259.0 1.3 collective-permute-start.7
  260.3 3.4 collective-permute-start.8
  263.7 1.1 fusion.12
  264.8 8.7 %multiply_add_fusion = f32[32,64,2048]{2,1,0:T(8,128)} fusion(f32[64,2048]{1,0:T(8,128)S(1)} %get-tuple-element.58, f32[32,2048]{1,0:T(8,128)S(1)} %get-tuple-element.57, f32[64,2048]{1,0:T(8,128)S(1)} %get-tuple-element.56, f32[32,2048]{1,0:T(8,128)S(1)} %get-tuple-element.55), kind=kLoop, calls=%fused_computation.3 | loop fusion | flops 12582912 | bytes 18350080 | tf_op jit(solution)/shard_map/add | solution.py:198
  273.5 61.3 %collective-permute-done.7.rest_2_ = f32[4,128,512]{2,1,0:T(8,128)S(1)} collective-permute-done((f32[4,128,512]{2,1,0:T(8,128)}, f32[4,128,512]{2,1,0:T(8,128)S(1)}, u32[]{:S(2)}, u32[]{:S(2)}) %collective-permute-start.7) | collective-permute-done | bytes 1048608 | tf_op jit(solution)/shard_map/ppermute | solution.py:219
  334.8 2.1 collective-permute-start.3
  336.9 20.9 %collective-permute-done.8.rest_3_ = f32[4,128,512]{2,1,0:T(8,128)S(1)} collective-permute-done((f32[4,128,512]{2,1,0:T(8,128)}, f32[4,128,512]{2,1,0:T(8,128)S(1)}, u32[]{:S(2)}, u32[]{:S(2)}) %collective-permute-start.8) | collective-permute-done | bytes 1048608 | tf_op jit(solution)/shard_map/ppermute | solution.py:219
  357.8 2.6 collective-permute-start.4
  360.4 0.0 collective-permute-done.9.rest_1_
  360.4 0.3 collective-permute-start.5
  360.8 0.0 collective-permute-done.10.rest_2_
  360.8 3.0 collective-permute-start
  363.8 0.0 collective-permute-done.11.rest_3_
  363.8 0.3 collective-permute-start.1
  364.1 12.4 %fusion = (bf16[2048,2048]{1,0:T(8,128)(2,1)}, bf16[2048,2048]{1,0:T(8,128)(2,1)}) fusion(f32[32,64,2048]{2,1,0:T(8,128)} %multiply_add_fusion), kind=kLoop, calls=%fused_computation.2 | loop fusion | flops 16777216 | bytes 33554432 | tf_op jit(solution)/shard_map/convert_element_type | solution.py:182
  376.5 0.1 dynamic-slice_bitcast_fusion
  376.6 0.7 copy.29.part_y
  377.3 1.3 dynamic_slice.6.part_x
  378.7 9.8 %z_modes.7.rest_1_ = f32[2,128,2048]{2,1,0:T(8,128)} custom-call(f32[16]{0:T(128)} %dynamic_slice.6.part_x, bf16[2048,2048]{1,0:T(8,128)(2,1)} %get-tuple-element.88.high, bf16[2048,2048]{1,0:T(8,128)(2,1)} %get-tuple-element.87.low, f32[128,1]{1,0:T(8,128)} %copy.29.part_y, f32[1,2048]{1,0:T(1,128)} %bitcast.10, f32[2,128,512]{2,1,0:T(8,128)} %get-tuple-element.67.rest_0_, ...), custom_call_target="tpu_custom_call" | custom-call | tf_op jit(solution)/shard_map/z_modes/pallas_call | solution.py:168
  388.5 14.0 %z_modes.8.rest_4_ = f32[16,128,2048]{2,1,0:T(8,128)} custom-call(f32[16]{0:T(128)} %dynamic_slice.6.part_x, bf16[2048,2048]{1,0:T(8,128)(2,1)} %get-tuple-element.88.high, bf16[2048,2048]{1,0:T(8,128)(2,1)} %get-tuple-element.87.low, f32[128,1]{1,0:T(8,128)} %copy.29.part_y, f32[1,2048]{1,0:T(1,128)} %bitcast.11, f32[2,128,512]{2,1,0:T(8,128)} %get-tuple-element.81.rest_0_, ...), custom_call_target="tpu_custom_call" | custom-call | tf_op jit(solution)/shard_map/z_modes/pallas_call | solution.py:168
  402.5 23.1 %z_modes.9.rest_4_ = f32[16,128,2048]{2,1,0:T(8,128)} custom-call(f32[16]{0:T(128)} %dynamic_slice.6.part_x, bf16[2048,2048]{1,0:T(8,128)(2,1)} %get-tuple-element.88.high, bf16[2048,2048]{1,0:T(8,128)(2,1)} %get-tuple-element.87.low, f32[128,1]{1,0:T(8,128)} %copy.29.part_y, f32[1,2048]{1,0:T(1,128)} %bitcast.12, ...), custom_call_target="tpu_custom_call", output_to_operand_aliasing={{}: (9, {})} | custom-call | tf_op jit(solution)/shard_map/z_modes/pallas_call | solution.py:168
  425.6 19.3 %z_modes.10.rest_4_ = f32[16,128,2048]{2,1,0:T(8,128)} custom-call(f32[16]{0:T(128)} %dynamic_slice.6.part_x, bf16[2048,2048]{1,0:T(8,128)(2,1)} %get-tuple-element.88.high, bf16[2048,2048]{1,0:T(8,128)(2,1)} %get-tuple-element.87.low, f32[128,1]{1,0:T(8,128)} %copy.29.part_y, f32[1,2048]{1,0:T(1,128)} %bitcast.13, ...), custom_call_target="tpu_custom_call", output_to_operand_aliasing={{}: (9, {})} | custom-call | tf_op jit(solution)/shard_map/z_modes/pallas_call | solution.py:168
  444.9 0.0 collective-permute-done.3.rest_1_
  445.0 0.9 copy-done.6
  445.8 16.4 %z_modes.11.rest_2_ = f32[16,128,2048]{2,1,0:T(8,128)} custom-call(f32[16]{0:T(128)} %dynamic_slice.6.part_x, bf16[2048,2048]{1,0:T(8,128)(2,1)} %get-tuple-element.88.high, bf16[2048,2048]{1,0:T(8,128)(2,1)} %get-tuple-element.87.low, f32[128,1]{1,0:T(8,128)} %copy.29.part_y, f32[1,2048]{1,0:T(1,128)} %bitcast.14, ...), custom_call_target="tpu_custom_call", output_to_operand_aliasing={{}: (9, {})} | custom-call | tf_op jit(solution)/shard_map/z_modes/pallas_call | solution.py:168
  462.3 6.2 %z_modes.12.rest_1_ = f32[2,128,2048]{2,1,0:T(8,128)} custom-call(f32[16]{0:T(128)} %dynamic_slice.6.part_x, bf16[2048,2048]{1,0:T(8,128)(2,1)} %get-tuple-element.88.high, bf16[2048,2048]{1,0:T(8,128)(2,1)} %get-tuple-element.87.low, f32[128,1]{1,0:T(8,128)} %copy.29.part_y, f32[1,2048]{1,0:T(1,128)} %bitcast.15, ...), custom_call_target="tpu_custom_call" | custom-call | tf_op jit(solution)/shard_map/z_modes/pallas_call | solution.py:168
  468.5 6.2 %z_modes.13 = f32[16,128,2048]{2,1,0:T(8,128)} custom-call(f32[16]{0:T(128)} %dynamic_slice.6.part_x, bf16[2048,2048]{1,0:T(8,128)(2,1)} %get-tuple-element.88.high, bf16[2048,2048]{1,0:T(8,128)(2,1)} %get-tuple-element.87.low, f32[128,1]{1,0:T(8,128)} %copy.29.part_y, f32[1,2048]{1,0:T(1,128)} %bitcast.16, ...), custom_call_target="tpu_custom_call", output_to_operand_aliasing={{}: (7, {})} | custom-call | tf_op jit(solution)/shard_map/z_modes/pallas_call | solution.py:168
  (29 shorter events, 0.1 us)
Async XLA Ops:
  0.0 376.5 %copy-start = (f32[512]{0:T(512)S(1)}, f32[512]{0:T(512)}, u32[]{:S(2)}) copy-start(f32[512]{0:T(512)} %param.20) | copy-start | bytes 6148
  212.4 17.8 %copy-start.11 = (f32[2,128,512]{2,1,0:T(8,128)S(1)}, f32[2,128,512]{2,1,0:T(8,128)}, u32[]{:S(2)}) copy-start(f32[2,128,512]{2,1,0:T(8,128)} %get-tuple-element.82) | copy-start | bytes 1572868
  212.4 17.9 %copy-start.10 = (f32[2,128,512]{2,1,0:T(8,128)S(1)}, f32[2,128,512]{2,1,0:T(8,128)}, u32[]{:S(2)}) copy-start(f32[2,128,512]{2,1,0:T(8,128)} %get-tuple-element.83) | copy-start | bytes 1572868
  228.0 32.3 %collective-permute-start.6 = (f32[4,128,512]{2,1,0:T(8,128)}, f32[4,128,512]{2,1,0:T(8,128)}, u32[]{:S(2)}, u32[]{:S(2)}) collective-permute-start(f32[4,128,512]{2,1,0:T(8,128)} %get-tuple-element.74), channel_id=1, source_target_pairs={{0,1},{1,0},{2,3},{3,2},{4,5},{5,4},{6,7},{7,6},{8,9},{9,8},{10,11... | collective-permute-start | bytes 3145736 | tf_op jit(solution)/shard_map/ppermute | solution.py:219
  230.2 16.1 %collective-permute-start.12 = (f32[2,128,512]{2,1,0:T(8,128)S(1)}, f32[2,128,512]{2,1,0:T(8,128)S(1)}, u32[]{:S(2)}, u32[]{:S(2)}) collective-permute-start(f32[2,128,512]{2,1,0:T(8,128)S(1)} %copy-done.11), channel_id=1, source_target_pairs={{0,1},{1,0},{2,3},{3,2},{4,5},{5,4},{6,7},{7,6},{8,9},{9,8},{10,11... | collective-permute-start | bytes 1572872 | tf_op jit(solution)/shard_map/ppermute | solution.py:219
  230.3 17.4 %collective-permute-start.13 = (f32[2,128,512]{2,1,0:T(8,128)S(1)}, f32[2,128,512]{2,1,0:T(8,128)S(1)}, u32[]{:S(2)}, u32[]{:S(2)}) collective-permute-start(f32[2,128,512]{2,1,0:T(8,128)S(1)} %copy-done.10), channel_id=1, source_target_pairs={{0,2},{1,3},{2,0},{3,1},{4,6},{5,7},{6,4},{7,5},{8,10},{9,11},{10,... | collective-permute-start | bytes 1572872 | tf_op jit(solution)/shard_map/ppermute | solution.py:219
  232.9 24.6 %collective-permute-start.14 = (f32[2,128,512]{2,1,0:T(8,128)}, f32[2,128,512]{2,1,0:T(8,128)S(1)}, u32[]{:S(2)}, u32[]{:S(2)}) collective-permute-start(f32[2,128,512]{2,1,0:T(8,128)} %get-tuple-element.84), channel_id=1, source_target_pairs={{0,3},{1,2},{2,1},{3,0},{4,7},{5,6},{6,5},{7,4},{8,11},{9,10},{10,... | collective-permute-start | bytes 1572872 | tf_op jit(solution)/shard_map/ppermute | solution.py:219
  244.2 14.8 %collective-permute-start.2 = (f32[2,128,512]{2,1,0:T(8,128)}, f32[2,128,512]{2,1,0:T(8,128)}, u32[]{:S(2)}, u32[]{:S(2)}) collective-permute-start(f32[2,128,512]{2,1,0:T(8,128)} %get-tuple-element.68), channel_id=1, source_target_pairs={{0,1},{1,0},{2,3},{3,2},{4,5},{5,4},{6,7},{7,6},{8,9},{9,8},{10,11... | collective-permute-start | bytes 1572872 | tf_op jit(solution)/shard_map/ppermute | solution.py:219
  246.4 0.8 copy-start.7
  247.2 113.3 %collective-permute-start.9 = (f32[5,128,512]{2,1,0:T(8,128)}, f32[5,128,512]{2,1,0:T(8,128)S(1)}, u32[]{:S(2)}, u32[]{:S(2)}) collective-permute-start(f32[5,128,512]{2,1,0:T(8,128)} %get-tuple-element.78), channel_id=1, source_target_pairs={{0,1},{1,0},{2,3},{3,2},{4,5},{5,4},{6,7},{7,6},{8,9},{9,8},{10,11... | collective-permute-start | bytes 3932168 | tf_op jit(solution)/shard_map/ppermute | solution.py:219
  247.7 0.8 copy-start.8
  248.5 112.3 %collective-permute-start.10 = (f32[5,128,512]{2,1,0:T(8,128)}, f32[5,128,512]{2,1,0:T(8,128)S(1)}, u32[]{:S(2)}, u32[]{:S(2)}) collective-permute-start(f32[5,128,512]{2,1,0:T(8,128)} %get-tuple-element.79), channel_id=1, source_target_pairs={{0,2},{1,3},{2,0},{3,1},{4,6},{5,7},{6,4},{7,5},{8,10},{9,11},{10,... | collective-permute-start | bytes 3932168 | tf_op jit(solution)/shard_map/ppermute | solution.py:219
  257.6 77.2 %copy-start.9 = (f32[2,128,512]{2,1,0:T(8,128)}, f32[2,128,512]{2,1,0:T(8,128)S(1)}, u32[]{:S(2)}) copy-start(f32[2,128,512]{2,1,0:T(8,128)S(1)} %collective-permute-done.14.rest_3_) | copy-start | bytes 1572868
  257.6 106.2 %collective-permute-start.11 = (f32[5,128,512]{2,1,0:T(8,128)}, f32[5,128,512]{2,1,0:T(8,128)}, u32[]{:S(2)}, u32[]{:S(2)}) collective-permute-start(f32[5,128,512]{2,1,0:T(8,128)} %get-tuple-element.80), channel_id=1, source_target_pairs={{0,3},{1,2},{2,1},{3,0},{4,7},{5,6},{6,5},{7,4},{8,11},{9,10},{10,... | collective-permute-start | bytes 3932168 | tf_op jit(solution)/shard_map/ppermute | solution.py:219
  259.0 75.7 %collective-permute-start.7 = (f32[4,128,512]{2,1,0:T(8,128)}, f32[4,128,512]{2,1,0:T(8,128)S(1)}, u32[]{:S(2)}, u32[]{:S(2)}) collective-permute-start(f32[4,128,512]{2,1,0:T(8,128)} %get-tuple-element.75), channel_id=1, source_target_pairs={{0,2},{1,3},{2,0},{3,1},{4,6},{5,7},{6,4},{7,5},{8,10},{9,11},{10,... | collective-permute-start | bytes 3145736 | tf_op jit(solution)/shard_map/ppermute | solution.py:219
  260.3 97.5 %collective-permute-start.8 = (f32[4,128,512]{2,1,0:T(8,128)}, f32[4,128,512]{2,1,0:T(8,128)S(1)}, u32[]{:S(2)}, u32[]{:S(2)}) collective-permute-start(f32[4,128,512]{2,1,0:T(8,128)} %get-tuple-element.76), channel_id=1, source_target_pairs={{0,3},{1,2},{2,1},{3,0},{4,7},{5,6},{6,5},{7,4},{8,11},{9,10},{10,... | collective-permute-start | bytes 3145736 | tf_op jit(solution)/shard_map/ppermute | solution.py:219
  334.8 26.0 %copy-start.4 = (f32[4,128,512]{2,1,0:T(8,128)}, f32[4,128,512]{2,1,0:T(8,128)S(1)}, u32[]{:S(2)}) copy-start(f32[4,128,512]{2,1,0:T(8,128)S(1)} %collective-permute-done.7.rest_2_) | copy-start | bytes 3145732
  334.8 110.2 %collective-permute-start.3 = (f32[3,128,512]{2,1,0:T(8,128)}, f32[3,128,512]{2,1,0:T(8,128)S(1)}, u32[]{:S(2)}, u32[]{:S(2)}) collective-permute-start(f32[3,128,512]{2,1,0:T(8,128)} %get-tuple-element.70), channel_id=1, source_target_pairs={{0,1},{1,0},{2,3},{3,2},{4,5},{5,4},{6,7},{7,6},{8,9},{9,8},{10,11... | collective-permute-start | bytes 2359304 | tf_op jit(solution)/shard_map/ppermute | solution.py:219
  357.8 3.0 copy-start.5
  357.8 87.1 %collective-permute-start.4 = (f32[3,128,512]{2,1,0:T(8,128)}, f32[3,128,512]{2,1,0:T(8,128)}, u32[]{:S(2)}, u32[]{:S(2)}) collective-permute-start(f32[3,128,512]{2,1,0:T(8,128)} %get-tuple-element.71), channel_id=1, source_target_pairs={{0,2},{1,3},{2,0},{3,1},{4,6},{5,7},{6,4},{7,5},{8,10},{9,11},{10,... | collective-permute-start | bytes 2359304 | tf_op jit(solution)/shard_map/ppermute | solution.py:219
  360.4 16.1 %copy-start.2 = (f32[5,128,512]{2,1,0:T(8,128)}, f32[5,128,512]{2,1,0:T(8,128)S(1)}, u32[]{:S(2)}) copy-start(f32[5,128,512]{2,1,0:T(8,128)S(1)} %collective-permute-done.9.rest_1_) | copy-start | bytes 3932164
  360.4 84.5 %collective-permute-start.5 = (f32[3,128,512]{2,1,0:T(8,128)}, f32[3,128,512]{2,1,0:T(8,128)}, u32[]{:S(2)}, u32[]{:S(2)}) collective-permute-start(f32[3,128,512]{2,1,0:T(8,128)} %get-tuple-element.72), channel_id=1, source_target_pairs={{0,3},{1,2},{2,1},{3,0},{4,7},{5,6},{6,5},{7,4},{8,11},{9,10},{10,... | collective-permute-start | bytes 2359304 | tf_op jit(solution)/shard_map/ppermute | solution.py:219
  360.8 15.7 %copy-start.3 = (f32[5,128,512]{2,1,0:T(8,128)}, f32[5,128,512]{2,1,0:T(8,128)S(1)}, u32[]{:S(2)}) copy-start(f32[5,128,512]{2,1,0:T(8,128)S(1)} %collective-permute-done.10.rest_2_) | copy-start | bytes 3932164
  360.8 107.7 %collective-permute-start = (f32[2,128,512]{2,1,0:T(8,128)}, f32[2,128,512]{2,1,0:T(8,128)}, u32[]{:S(2)}, u32[]{:S(2)}) collective-permute-start(f32[2,128,512]{2,1,0:T(8,128)} %get-tuple-element.64), channel_id=1, source_target_pairs={{0,3},{1,2},{2,1},{3,0},{4,7},{5,6},{6,5},{7,4},{8,11},{9,10},{10,... | collective-permute-start | bytes 1572872 | tf_op jit(solution)/shard_map/ppermute | solution.py:219
  363.8 98.5 %collective-permute-start.1 = (f32[2,128,512]{2,1,0:T(8,128)}, f32[2,128,512]{2,1,0:T(8,128)}, u32[]{:S(2)}, u32[]{:S(2)}) collective-permute-start(f32[2,128,512]{2,1,0:T(8,128)} %get-tuple-element.65), channel_id=1, source_target_pairs={{0,2},{1,3},{2,0},{3,1},{4,6},{5,7},{6,4},{7,5},{8,10},{9,11},{10,... | collective-permute-start | bytes 1572872 | tf_op jit(solution)/shard_map/ppermute | solution.py:219
  444.9 0.9 copy-start.6
  462.2 12.4 %copy-start.1 = (f32[512]{0:T(512)S(1)}, f32[512]{0:T(512)}, u32[]{:S(2)}) copy-start(f32[512]{0:T(512)} %param.20) | copy-start | bytes 6148
where the time goes:
time: 476 us; the launch traced here: 475 us
  blocking collectives  194 us (41%)
  Pallas kernels  140 us (29%)
  waiting for transfers between devices  88.7 us (19%)
  other arithmetic  24.3 us (5%)
  starting transfers between devices  23.6 us (5%)
    all_to_all x1, blocking collectives, per_device(): a = lax.all_to_all(a, 'left', split_axis=0, concat_axis=0, tiled=True)  194 us
    pallas_call x7, Pallas kernels, z_modes(): pl.pallas_call(functools.partial(z_kernel, lo=lo, count=count, summed=sum...  95 us
    ppermute x15, waiting for transfers between devices, per_device(): met.append(lax.ppermute(b[k], 'right', [(r, r ^ k) for r in range(right)]))  88.7 us
    pallas_call x5, Pallas kernels, y_modes(): pl.pallas_call(functools.partial(y_kernel, right=right), grid_spec=pltpu....  30.4 us
    ppermute x15, starting transfers between devices, per_device(): met.append(lax.ppermute(b[k], 'right', [(r, r ^ k) for r in range(right)]))  23.6 us
    pallas_call x1, Pallas kernels, x_modes(): pl.pallas_call(x_kernel, grid=(ny // rows, nz // lanes), in_specs=[block,...  14.3 us
    convert_element_type x1, other arithmetic, run_halves(): return (high.astype(BF16), (table - high).astype(BF16))  12.4 us
  transfers between devices with their start and end apart: 15, of which 3 were waited for; matrix products, arithmetic and copies ran while one was open for 6% of the time, Pallas kernels for 21%

commit v1 on v0

--- a/solution.py
+++ b/solution.py
@@ -8,7 +8,7 @@
 from jax.experimental.pallas import tpu as pltpu
 from jax.sharding import PartitionSpec as P
 
-CUTS = (0, 2, 7, 11, 14, 16)
+CUTS = (0, 1, 3, 8, 12, 14, 16)
 F32 = jnp.float32
 BF16 = jnp.bfloat16
 
@@ -173,6 +173,7 @@
         out_shape=jax.ShapeDtypeStruct((part_x.shape[0] if last else own, share, nz), F32),
         scratch_shapes=[pltpu.VMEM((2 * own * share, count * width), BF16)],
         input_output_aliases=aliases,
+        compiler_params=pltpu.CompilerParams(vmem_limit_bytes=(59 if last and sums is None else 52) * 2**20),
         name="z_modes",
     )(*args)
 
@@ -218,7 +219,7 @@
         for k in range(1, right):
             met.append(lax.ppermute(b[k], "right", [(r, r ^ k) for r in range(right)]))
         sent.append(met)
-        if c == 1:
+        if c == 2:
             at = at_right[0] + zero
             tables = z_tables(nz_part * right, right, at, zero)
             part_x = lax.dynamic_slice_in_dim(symbol_x, at_left * share_x, share_x)

time: 476 us -> 501 us (1.053)
  Pallas kernels: 140 us -> 150 us
  waiting for transfers between devices: 88.7 us -> 98 us
    ppermute x15 -> x18, waiting for transfers between devices: 88.7 us -> 98 us  [per_device(): met.append(lax.ppermute(b[k], 'right', [(r, r ^ k) for r in range(right)]))]
    pallas_call x7 -> x8, Pallas kernels: 95 us -> 103 us  [z_modes(): pl.pallas_call(functools.partial(z_kernel, lo=lo, count=count, summed=sum...]
    ppermute x15 -> x18, starting transfers between devices: 23.6 us -> 27.8 us  [per_device(): met.append(lax.ppermute(b[k], 'right', [(r, r ^ k) for r in range(right)]))]
    pallas_call x5 -> x6, Pallas kernels: 30.4 us -> 32.4 us  [y_modes(): pl.pallas_call(functools.partial(y_kernel, right=right), grid_spec=pltpu....]
  transfers between devices with their start and end apart: 15 -> 18, of which waited for: 3 -> 4; matrix products, arithmetic and copies ran while one was open for 6% -> 5% of each run, Pallas kernels for 21% -> 21%
where the time goes in v1:
time: 501 us; the launch traced here: 500 us
  blocking collectives  194 us (39%)
  Pallas kernels  150 us (30%)
  waiting for transfers between devices  98 us (20%)
  starting transfers between devices  27.8 us (6%)
  other arithmetic  24.3 us (5%)
  local copies, waits for them, and re-layouts  5.86 us (1%)
    all_to_all x1, blocking collectives, per_device(): a = lax.all_to_all(a, 'left', split_axis=0, concat_axis=0, tiled=True)  194 us
    pallas_call x8, Pallas kernels, z_modes(): pl.pallas_call(functools.partial(z_kernel, lo=lo, count=count, summed=sum...  103 us
    ppermute x18, waiting for transfers between devices, per_device(): met.append(lax.ppermute(b[k], 'right', [(r, r ^ k) for r in range(right)]))  98 us
    pallas_call x6, Pallas kernels, y_modes(): pl.pallas_call(functools.partial(y_kernel, right=right), grid_spec=pltpu....  32.4 us
    ppermute x18, starting transfers between devices, per_device(): met.append(lax.ppermute(b[k], 'right', [(r, r ^ k) for r in range(right)]))  27.8 us
    pallas_call x1, Pallas kernels, x_modes(): pl.pallas_call(x_kernel, grid=(ny // rows, nz // lanes), in_specs=[block,...  14.3 us
    convert_element_type x1, other arithmetic, run_halves(): return (high.astype(BF16), (table - high).astype(BF16))  12.4 us
  transfers between devices with their start and end apart: 18, of which 4 were waited for; matrix products, arithmetic and copies ran while one was open for 5% of the time, Pallas kernels for 21%

profile of v1, /device:TPU:1, one launch (start us, length us, event | category | flops | bytes accessed | tf_op | source)
XLA Modules:
  0.0 499.5 jit_solution(9527033868843126136)
XLA Ops:
  0.0 14.3 %x_modes.1 = f32[512,16,512]{2,1,0:T(8,128)S(1)} custom-call(f32[512,16,512]{2,1,0:T(8,128)} %values.1, bf16[4,256,256]{2,1,0:T(8,128)(2,1)} %constant.95.tables), custom_call_target="tpu_custom_call" | custom-call | tf_op jit(solution)/shard_map/x_modes/pallas_call | solution.py:77
  14.3 193.6 %all_to_all.5.values = f32[32,16,16,512]{3,2,1,0:T(8,128)} all-to-all(f32[32,16,16,512]{3,2,1,0:T(8,128)S(1)} %bitcast.9), channel_id=1, replica_groups=mesh['left'=32,'right'=4] {'left'}, dimensions={0} | all-to-all | bytes 33554432 | tf_op jit(solution)/shard_map/all_to_all | solution.py:213
  207.9 3.4 y_modes.6
  211.3 4.5 y_modes.7
  215.8 8.6 %y_modes.8 = (f32[5,128,512]{2,1,0:T(8,128)}, f32[5,128,512]{2,1,0:T(8,128)}, f32[5,128,512]{2,1,0:T(8,128)}, f32[5,128,512]{2,1,0:T(8,128)}) custom-call(s32[1]{0:T(128)} %bitcast.1.own, f32[32,16,16,512]{3,2,1,0:T(8,128)} %all_to_all.5.values, bf16[512,512]{1,0:T(8,128)(2,1)} %constant.88.clone.rest_0_.rest_1_.rest_2_.rest_3_, ...), custom_call_target="tpu_custom_call" | custom-call | tf_op jit(solution)/shard_map/y_modes/pallas_call | solution.py:106
  224.4 7.0 %y_modes.9 = (f32[4,128,512]{2,1,0:T(8,128)}, f32[4,128,512]{2,1,0:T(8,128)}, f32[4,128,512]{2,1,0:T(8,128)}, f32[4,128,512]{2,1,0:T(8,128)}) custom-call(s32[1]{0:T(128)} %bitcast.1.own, f32[32,16,16,512]{3,2,1,0:T(8,128)} %all_to_all.5.values, bf16[512,512]{1,0:T(8,128)(2,1)} %constant.88.clone.rest_0_.rest_1_.rest_2_.rest_3_, ...), custom_call_target="tpu_custom_call" | custom-call | tf_op jit(solution)/shard_map/y_modes/pallas_call | solution.py:106
  231.4 2.2 collective-permute-start.6
  233.6 0.1 collective-permute-start.15
  233.7 2.6 collective-permute-start.16
  236.3 0.9 collective-permute-start.17
  237.3 4.5 y_modes.10
  241.8 4.5 y_modes.11
  246.3 2.7 collective-permute-start.13
  249.0 1.0 collective-permute-start.14
  250.0 0.4 collective-permute-start.2
  250.4 2.1 fusion.7
  252.6 0.2 collective-permute-start.9
  252.8 8.3 %collective-permute-done.13.rest_2_ = f32[2,128,512]{2,1,0:T(8,128)S(1)} collective-permute-done((f32[2,128,512]{2,1,0:T(8,128)}, f32[2,128,512]{2,1,0:T(8,128)S(1)}, u32[]{:S(2)}, u32[]{:S(2)}) %collective-permute-start.13) | collective-permute-done | bytes 524320 | tf_op jit(solution)/shard_map/ppermute | solution.py:220
  261.1 0.8 copy-done.16
  261.9 2.6 collective-permute-start.10
  264.5 9.3 %collective-permute-done.14.rest_3_ = f32[2,128,512]{2,1,0:T(8,128)S(1)} collective-permute-done((f32[2,128,512]{2,1,0:T(8,128)}, f32[2,128,512]{2,1,0:T(8,128)S(1)}, u32[]{:S(2)}, u32[]{:S(2)}) %collective-permute-start.14) | collective-permute-done | bytes 524320 | tf_op jit(solution)/shard_map/ppermute | solution.py:220
  273.9 0.8 copy-done.17
  274.6 1.4 collective-permute-start.11
  276.0 1.3 collective-permute-start.7
  277.3 1.0 copy-done.12
  278.2 3.5 collective-permute-start.8
  281.8 1.1 fusion.12
  282.9 8.7 %multiply_add_fusion = f32[32,64,2048]{2,1,0:T(8,128)} fusion(f32[64,2048]{1,0:T(8,128)S(1)} %get-tuple-element.68, f32[32,2048]{1,0:T(8,128)S(1)} %get-tuple-element.67, f32[64,2048]{1,0:T(8,128)S(1)} %get-tuple-element.66, f32[32,2048]{1,0:T(8,128)S(1)} %get-tuple-element.65), kind=kLoop, calls=%fused_computation.3 | loop fusion | flops 12582912 | bytes 18350080 | tf_op jit(solution)/shard_map/add | solution.py:199
  291.5 59.4 %collective-permute-done.7.rest_2_ = f32[4,128,512]{2,1,0:T(8,128)S(1)} collective-permute-done((f32[4,128,512]{2,1,0:T(8,128)}, f32[4,128,512]{2,1,0:T(8,128)S(1)}, u32[]{:S(2)}, u32[]{:S(2)}) %collective-permute-start.7) | collective-permute-done | bytes 1048608 | tf_op jit(solution)/shard_map/ppermute | solution.py:220
  351.0 2.2 collective-permute-start.3
  353.2 20.9 %collective-permute-done.8.rest_3_ = f32[4,128,512]{2,1,0:T(8,128)S(1)} collective-permute-done((f32[4,128,512]{2,1,0:T(8,128)}, f32[4,128,512]{2,1,0:T(8,128)S(1)}, u32[]{:S(2)}, u32[]{:S(2)}) %collective-permute-start.8) | collective-permute-done | bytes 1048608 | tf_op jit(solution)/shard_map/ppermute | solution.py:220
  374.1 2.6 collective-permute-start.4
  376.7 0.3 collective-permute-start.5
  377.0 3.0 collective-permute-start
  380.0 1.1 copy-done.11
  381.0 0.7 collective-permute-start.1
  381.8 12.4 %fusion = (bf16[2048,2048]{1,0:T(8,128)(2,1)}, bf16[2048,2048]{1,0:T(8,128)(2,1)}) fusion(f32[32,64,2048]{2,1,0:T(8,128)} %multiply_add_fusion), kind=kLoop, calls=%fused_computation.2 | loop fusion | flops 16777216 | bytes 33554432 | tf_op jit(solution)/shard_map/convert_element_type | solution.py:183
  394.1 0.1 dynamic-slice_bitcast_fusion
  394.2 0.7 copy.33.part_y
  395.0 1.3 dynamic_slice.6.part_x
  396.3 11.6 %z_modes.9.rest_4_ = f32[16,128,2048]{2,1,0:T(8,128)} custom-call(f32[16]{0:T(128)} %dynamic_slice.6.part_x, bf16[2048,2048]{1,0:T(8,128)(2,1)} %get-tuple-element.102.high, bf16[2048,2048]{1,0:T(8,128)(2,1)} %get-tuple-element.101.low, f32[128,1]{1,0:T(8,128)} %copy.33.part_y, f32[1,2048]{1,0:T(1,128)} %bitcast.10, ...), custom_call_target="tpu_custom_call" | custom-call | tf_op jit(solution)/shard_map/z_modes/pallas_call | solution.py:168
  408.0 9.3 %z_modes.8.rest_1_ = f32[2,128,2048]{2,1,0:T(8,128)} custom-call(f32[16]{0:T(128)S(1)} %copy-done.7, bf16[2048,2048]{1,0:T(8,128)(2,1)} %get-tuple-element.102.high, bf16[2048,2048]{1,0:T(8,128)(2,1)} %get-tuple-element.101.low, f32[128,1]{1,0:T(8,128)S(1)} %copy-done.2, f32[1,2048]{1,0:T(1,128)S(1)} %bitcast.15, f32[2,128,512]{2,1,0:T(8,128)S(1)} %copy-done.4, ...), custom_call_target="tpu_custom_call" | custom-call | tf_op jit(solution)/shard_map/z_modes/pallas_call | solution.py:168
  417.2 14.0 %z_modes.10.rest_4_ = f32[16,128,2048]{2,1,0:T(8,128)} custom-call(f32[16]{0:T(128)} %dynamic_slice.6.part_x, bf16[2048,2048]{1,0:T(8,128)(2,1)} %get-tuple-element.102.high, bf16[2048,2048]{1,0:T(8,128)(2,1)} %get-tuple-element.101.low, f32[128,1]{1,0:T(8,128)} %copy.33.part_y, f32[1,2048]{1,0:T(1,128)} %bitcast.11, ...), custom_call_target="tpu_custom_call", output_to_operand_aliasing={{}: (9, {})} | custom-call | tf_op jit(solution)/shard_map/z_modes/pallas_call | solution.py:168
  431.3 23.1 %z_modes.11.rest_4_ = f32[16,128,2048]{2,1,0:T(8,128)} custom-call(f32[16]{0:T(128)} %dynamic_slice.6.part_x, bf16[2048,2048]{1,0:T(8,128)(2,1)} %get-tuple-element.102.high, bf16[2048,2048]{1,0:T(8,128)(2,1)} %get-tuple-element.101.low, f32[128,1]{1,0:T(8,128)} %copy.33.part_y, f32[1,2048]{1,0:T(1,128)} %bitcast.12, ...), custom_call_target="tpu_custom_call", output_to_operand_aliasing={{}: (9, {})} | custom-call | tf_op jit(solution)/shard_map/z_modes/pallas_call | solution.py:168
  454.3 19.3 %z_modes.12.rest_4_ = f32[16,128,2048]{2,1,0:T(8,128)} custom-call(f32[16]{0:T(128)} %dynamic_slice.6.part_x, bf16[2048,2048]{1,0:T(8,128)(2,1)} %get-tuple-element.102.high, bf16[2048,2048]{1,0:T(8,128)(2,1)} %get-tuple-element.101.low, f32[128,1]{1,0:T(8,128)} %copy.33.part_y, f32[1,2048]{1,0:T(1,128)} %bitcast.13, ...), custom_call_target="tpu_custom_call", output_to_operand_aliasing={{}: (9, {})} | custom-call | tf_op jit(solution)/shard_map/z_modes/pallas_call | solution.py:168
  473.7 14.2 %z_modes.13.rest_2_ = f32[16,128,2048]{2,1,0:T(8,128)} custom-call(f32[16]{0:T(128)} %dynamic_slice.6.part_x, bf16[2048,2048]{1,0:T(8,128)(2,1)} %get-tuple-element.102.high, bf16[2048,2048]{1,0:T(8,128)(2,1)} %get-tuple-element.101.low, f32[128,1]{1,0:T(8,128)} %copy.33.part_y, f32[1,2048]{1,0:T(1,128)} %bitcast.14, ...), custom_call_target="tpu_custom_call", output_to_operand_aliasing={{}: (9, {})} | custom-call | tf_op jit(solution)/shard_map/z_modes/pallas_call | solution.py:168
  487.9 5.8 %z_modes.14.rest_1_ = f32[2,128,2048]{2,1,0:T(8,128)} custom-call(f32[16]{0:T(128)S(1)} %copy-done.8, bf16[2048,2048]{1,0:T(8,128)(2,1)} %get-tuple-element.102.high, bf16[2048,2048]{1,0:T(8,128)(2,1)} %get-tuple-element.101.low, f32[128,1]{1,0:T(8,128)S(1)} %copy-done.3, f32[1,2048]{1,0:T(1,128)S(1)} %bitcast.16, ...), custom_call_target="tpu_custom_call" | custom-call | tf_op jit(solution)/shard_map/z_modes/pallas_call | solution.py:168
  493.7 5.8 %z_modes.15 = f32[16,128,2048]{2,1,0:T(8,128)} custom-call(f32[16]{0:T(128)S(1)} %copy-done.8, bf16[2048,2048]{1,0:T(8,128)(2,1)} %get-tuple-element.102.high, bf16[2048,2048]{1,0:T(8,128)(2,1)} %get-tuple-element.101.low, f32[128,1]{1,0:T(8,128)S(1)} %copy-done.3, f32[1,2048]{1,0:T(1,128)S(1)} %bitcast.17, ...), custom_call_target="tpu_custom_call", output_to_operand_aliasing={{}: (7, {})} | custom-call | tf_op jit(solution)/shard_map/z_modes/pallas_call | solution.py:168
  (61 shorter events, 0.1 us)
Async XLA Ops:
  0.0 394.1 %copy-start = (f32[512]{0:T(512)S(1)}, f32[512]{0:T(512)}, u32[]{:S(2)}) copy-start(f32[512]{0:T(512)} %param.22) | copy-start | bytes 6148
  215.8 17.9 %copy-start.23 = (f32[1,128,512]{2,1,0:T(8,128)S(1)}, f32[1,128,512]{2,1,0:T(8,128)}, u32[]{:S(2)}) copy-start(f32[1,128,512]{2,1,0:T(8,128)} %get-tuple-element.97) | copy-start | bytes 786436
  215.8 20.5 %copy-start.22 = (f32[1,128,512]{2,1,0:T(8,128)S(1)}, f32[1,128,512]{2,1,0:T(8,128)}, u32[]{:S(2)}) copy-start(f32[1,128,512]{2,1,0:T(8,128)} %get-tuple-element.98) | copy-start | bytes 786436
  215.8 21.5 %copy-start.21 = (f32[2,128,512]{2,1,0:T(8,128)S(1)}, f32[2,128,512]{2,1,0:T(8,128)}, u32[]{:S(2)}) copy-start(f32[2,128,512]{2,1,0:T(8,128)} %get-tuple-element.92) | copy-start | bytes 1572868
  231.4 45.9 %collective-permute-start.6 = (f32[4,128,512]{2,1,0:T(8,128)}, f32[4,128,512]{2,1,0:T(8,128)S(1)}, u32[]{:S(2)}, u32[]{:S(2)}) collective-permute-start(f32[4,128,512]{2,1,0:T(8,128)} %get-tuple-element.84), channel_id=1, source_target_pairs={{0,1},{1,0},{2,3},{3,2},{4,5},{5,4},{6,7},{7,6},{8,9},{9,8},{10,11... | collective-permute-start | bytes 3145736 | tf_op jit(solution)/shard_map/ppermute | solution.py:220
  233.6 12.6 %collective-permute-start.15 = (f32[1,128,512]{2,1,0:T(8,128)}, f32[1,128,512]{2,1,0:T(8,128)S(1)}, u32[]{:S(2)}, u32[]{:S(2)}) collective-permute-start(f32[1,128,512]{2,1,0:T(8,128)} %get-tuple-element.96), channel_id=1, source_target_pairs={{0,1},{1,0},{2,3},{3,2},{4,5},{5,4},{6,7},{7,6},{8,9},{9,8},{10,11... | collective-permute-start | bytes 786440 | tf_op jit(solution)/shard_map/ppermute | solution.py:220
  233.7 15.3 %collective-permute-start.16 = (f32[1,128,512]{2,1,0:T(8,128)S(1)}, f32[1,128,512]{2,1,0:T(8,128)S(1)}, u32[]{:S(2)}, u32[]{:S(2)}) collective-permute-start(f32[1,128,512]{2,1,0:T(8,128)S(1)} %copy-done.23), channel_id=1, source_target_pairs={{0,2},{1,3},{2,0},{3,1},{4,6},{5,7},{6,4},{7,5},{8,10},{9,11},{10,... | collective-permute-start | bytes 786440 | tf_op jit(solution)/shard_map/ppermute | solution.py:220
  236.3 13.6 %collective-permute-start.17 = (f32[1,128,512]{2,1,0:T(8,128)S(1)}, f32[1,128,512]{2,1,0:T(8,128)S(1)}, u32[]{:S(2)}, u32[]{:S(2)}) collective-permute-start(f32[1,128,512]{2,1,0:T(8,128)S(1)} %copy-done.22), channel_id=1, source_target_pairs={{0,3},{1,2},{2,1},{3,0},{4,7},{5,6},{6,5},{7,4},{8,11},{9,10},{10,... | collective-permute-start | bytes 786440 | tf_op jit(solution)/shard_map/ppermute | solution.py:220
  237.3 15.3 %collective-permute-start.12 = (f32[2,128,512]{2,1,0:T(8,128)S(1)}, f32[2,128,512]{2,1,0:T(8,128)S(1)}, u32[]{:S(2)}, u32[]{:S(2)}) collective-permute-start(f32[2,128,512]{2,1,0:T(8,128)S(1)} %copy-done.21), channel_id=1, source_target_pairs={{0,1},{1,0},{2,3},{3,2},{4,5},{5,4},{6,7},{7,6},{8,9},{9,8},{10,11... | collective-permute-start | bytes 1572872 | tf_op jit(solution)/shard_map/ppermute | solution.py:220
  246.3 3.7 copy-start.18
  246.3 14.8 %collective-permute-start.13 = (f32[2,128,512]{2,1,0:T(8,128)}, f32[2,128,512]{2,1,0:T(8,128)S(1)}, u32[]{:S(2)}, u32[]{:S(2)}) collective-permute-start(f32[2,128,512]{2,1,0:T(8,128)} %get-tuple-element.93), channel_id=1, source_target_pairs={{0,2},{1,3},{2,0},{3,1},{4,6},{5,7},{6,4},{7,5},{8,10},{9,11},{10,... | collective-permute-start | bytes 1572872 | tf_op jit(solution)/shard_map/ppermute | solution.py:220
  249.0 1.0 copy-start.19
  249.0 24.9 %collective-permute-start.14 = (f32[2,128,512]{2,1,0:T(8,128)}, f32[2,128,512]{2,1,0:T(8,128)S(1)}, u32[]{:S(2)}, u32[]{:S(2)}) collective-permute-start(f32[2,128,512]{2,1,0:T(8,128)} %get-tuple-element.94), channel_id=1, source_target_pairs={{0,3},{1,2},{2,1},{3,0},{4,7},{5,6},{6,5},{7,4},{8,11},{9,10},{10,... | collective-permute-start | bytes 1572872 | tf_op jit(solution)/shard_map/ppermute | solution.py:220
  250.0 2.6 copy-start.20
  250.0 26.1 %collective-permute-start.2 = (f32[2,128,512]{2,1,0:T(8,128)}, f32[2,128,512]{2,1,0:T(8,128)S(1)}, u32[]{:S(2)}, u32[]{:S(2)}) collective-permute-start(f32[2,128,512]{2,1,0:T(8,128)} %get-tuple-element.78), channel_id=1, source_target_pairs={{0,1},{1,0},{2,3},{3,2},{4,5},{5,4},{6,7},{7,6},{8,9},{9,8},{10,11... | collective-permute-start | bytes 1572872 | tf_op jit(solution)/shard_map/ppermute | solution.py:220
  252.6 164.7 %copy-start.15 = (f32[2,128,512]{2,1,0:T(8,128)}, f32[2,128,512]{2,1,0:T(8,128)S(1)}, u32[]{:S(2)}) copy-start(f32[2,128,512]{2,1,0:T(8,128)S(1)} %collective-permute-done.12.rest_1_) | copy-start | bytes 1572868
  252.6 124.1 %collective-permute-start.9 = (f32[5,128,512]{2,1,0:T(8,128)}, f32[5,128,512]{2,1,0:T(8,128)S(1)}, u32[]{:S(2)}, u32[]{:S(2)}) collective-permute-start(f32[5,128,512]{2,1,0:T(8,128)} %get-tuple-element.88), channel_id=1, source_target_pairs={{0,1},{1,0},{2,3},{3,2},{4,5},{5,4},{6,7},{7,6},{8,9},{9,8},{10,11... | collective-permute-start | bytes 3932168 | tf_op jit(solution)/shard_map/ppermute | solution.py:220
  261.1 0.8 copy-start.16
  261.9 115.1 %collective-permute-start.10 = (f32[5,128,512]{2,1,0:T(8,128)}, f32[5,128,512]{2,1,0:T(8,128)S(1)}, u32[]{:S(2)}, u32[]{:S(2)}) collective-permute-start(f32[5,128,512]{2,1,0:T(8,128)} %get-tuple-element.89), channel_id=1, source_target_pairs={{0,2},{1,3},{2,0},{3,1},{4,6},{5,7},{6,4},{7,5},{8,10},{9,11},{10,... | collective-permute-start | bytes 3932168 | tf_op jit(solution)/shard_map/ppermute | solution.py:220
  273.9 0.8 copy-start.17
  274.6 105.3 %collective-permute-start.11 = (f32[5,128,512]{2,1,0:T(8,128)}, f32[5,128,512]{2,1,0:T(8,128)S(1)}, u32[]{:S(2)}, u32[]{:S(2)}) collective-permute-start(f32[5,128,512]{2,1,0:T(8,128)} %get-tuple-element.90), channel_id=1, source_target_pairs={{0,3},{1,2},{2,1},{3,0},{4,7},{5,6},{6,5},{7,4},{8,11},{9,10},{10,... | collective-permute-start | bytes 3932168 | tf_op jit(solution)/shard_map/ppermute | solution.py:220
  276.0 75.0 %collective-permute-start.7 = (f32[4,128,512]{2,1,0:T(8,128)}, f32[4,128,512]{2,1,0:T(8,128)S(1)}, u32[]{:S(2)}, u32[]{:S(2)}) collective-permute-start(f32[4,128,512]{2,1,0:T(8,128)} %get-tuple-element.85), channel_id=1, source_target_pairs={{0,2},{1,3},{2,0},{3,1},{4,6},{5,7},{6,4},{7,5},{8,10},{9,11},{10,... | collective-permute-start | bytes 3145736 | tf_op jit(solution)/shard_map/ppermute | solution.py:220
  277.3 1.0 copy-start.12
  278.2 95.8 %collective-permute-start.8 = (f32[4,128,512]{2,1,0:T(8,128)}, f32[4,128,512]{2,1,0:T(8,128)S(1)}, u32[]{:S(2)}, u32[]{:S(2)}) collective-permute-start(f32[4,128,512]{2,1,0:T(8,128)} %get-tuple-element.86), channel_id=1, source_target_pairs={{0,3},{1,2},{2,1},{3,0},{4,7},{5,6},{6,5},{7,4},{8,11},{9,10},{10,... | collective-permute-start | bytes 3145736 | tf_op jit(solution)/shard_map/ppermute | solution.py:220
  351.0 30.8 %copy-start.13 = (f32[4,128,512]{2,1,0:T(8,128)}, f32[4,128,512]{2,1,0:T(8,128)S(1)}, u32[]{:S(2)}) copy-start(f32[4,128,512]{2,1,0:T(8,128)S(1)} %collective-permute-done.7.rest_2_) | copy-start | bytes 3145732
  351.0 122.7 %collective-permute-start.3 = (f32[2,128,512]{2,1,0:T(8,128)}, f32[2,128,512]{2,1,0:T(8,128)}, u32[]{:S(2)}, u32[]{:S(2)}) collective-permute-start(f32[2,128,512]{2,1,0:T(8,128)} %get-tuple-element.80), channel_id=1, source_target_pairs={{0,1},{1,0},{2,3},{3,2},{4,5},{5,4},{6,7},{7,6},{8,9},{9,8},{10,11... | collective-permute-start | bytes 1572872 | tf_op jit(solution)/shard_map/ppermute | solution.py:220
  374.1 7.7 %copy-start.14 = (f32[4,128,512]{2,1,0:T(8,128)}, f32[4,128,512]{2,1,0:T(8,128)S(1)}, u32[]{:S(2)}) copy-start(f32[4,128,512]{2,1,0:T(8,128)S(1)} %collective-permute-done.8.rest_3_) | copy-start | bytes 3145732
  374.1 99.6 %collective-permute-start.4 = (f32[2,128,512]{2,1,0:T(8,128)}, f32[2,128,512]{2,1,0:T(8,128)}, u32[]{:S(2)}, u32[]{:S(2)}) collective-permute-start(f32[2,128,512]{2,1,0:T(8,128)} %get-tuple-element.81), channel_id=1, source_target_pairs={{0,2},{1,3},{2,0},{3,1},{4,6},{5,7},{6,4},{7,5},{8,10},{9,11},{10,... | collective-permute-start | bytes 1572872 | tf_op jit(solution)/shard_map/ppermute | solution.py:220
  376.7 17.4 %copy-start.9 = (f32[5,128,512]{2,1,0:T(8,128)}, f32[5,128,512]{2,1,0:T(8,128)S(1)}, u32[]{:S(2)}) copy-start(f32[5,128,512]{2,1,0:T(8,128)S(1)} %collective-permute-done.9.rest_1_) | copy-start | bytes 3932164
  376.7 97.0 %collective-permute-start.5 = (f32[2,128,512]{2,1,0:T(8,128)}, f32[2,128,512]{2,1,0:T(8,128)}, u32[]{:S(2)}, u32[]{:S(2)}) collective-permute-start(f32[2,128,512]{2,1,0:T(8,128)} %get-tuple-element.82), channel_id=1, source_target_pairs={{0,3},{1,2},{2,1},{3,0},{4,7},{5,6},{6,5},{7,4},{8,11},{9,10},{10,... | collective-permute-start | bytes 1572872 | tf_op jit(solution)/shard_map/ppermute | solution.py:220
  377.0 3.0 copy-start.10
  377.0 116.8 %collective-permute-start = (f32[2,128,512]{2,1,0:T(8,128)}, f32[2,128,512]{2,1,0:T(8,128)S(1)}, u32[]{:S(2)}, u32[]{:S(2)}) collective-permute-start(f32[2,128,512]{2,1,0:T(8,128)} %get-tuple-element.74), channel_id=1, source_target_pairs={{0,3},{1,2},{2,1},{3,0},{4,7},{5,6},{6,5},{7,4},{8,11},{9,10},{10,... | collective-permute-start | bytes 1572872 | tf_op jit(solution)/shard_map/ppermute | solution.py:220
  380.0 1.1 copy-start.11
  381.0 106.9 %collective-permute-start.1 = (f32[2,128,512]{2,1,0:T(8,128)}, f32[2,128,512]{2,1,0:T(8,128)S(1)}, u32[]{:S(2)}, u32[]{:S(2)}) collective-permute-start(f32[2,128,512]{2,1,0:T(8,128)} %get-tuple-element.75), channel_id=1, source_target_pairs={{0,2},{1,3},{2,0},{3,1},{4,6},{5,7},{6,4},{7,5},{8,10},{9,11},{10,... | collective-permute-start | bytes 1572872 | tf_op jit(solution)/shard_map/ppermute | solution.py:220
  396.3 11.7 %copy-start.2 = (f32[128,1]{1,0:T(8,128)S(1)}, f32[128,1]{1,0:T(8,128)}, u32[]{:S(2)}) copy-start(f32[128,1]{1,0:T(8,128)} %copy.33.part_y) | copy-start | bytes 1540
  396.3 11.7 %copy-start.4 = (f32[2,128,512]{2,1,0:T(8,128)S(1)}, f32[2,128,512]{2,1,0:T(8,128)}, u32[]{:S(2)}) copy-start(f32[2,128,512]{2,1,0:T(8,128)} %get-tuple-element.77.rest_0_) | copy-start | bytes 1572868
  396.3 11.7 %copy-start.5 = (f32[2048]{0:T(1024)S(1)}, f32[2048]{0:T(1024)}, u32[]{:S(2)}) copy-start(f32[2048]{0:T(1024)} %param.23) | copy-start | bytes 24580
  396.3 11.7 %copy-start.7 = (f32[16]{0:T(128)S(1)}, f32[16]{0:T(128)}, u32[]{:S(2)}) copy-start(f32[16]{0:T(128)} %dynamic_slice.6.part_x) | copy-start | bytes 196
  473.7 14.2 %copy-start.3 = (f32[128,1]{1,0:T(8,128)S(1)}, f32[128,1]{1,0:T(8,128)}, u32[]{:S(2)}) copy-start(f32[128,1]{1,0:T(8,128)} %copy.33.part_y) | copy-start | bytes 1540
  473.7 14.2 %copy-start.6 = (f32[2048]{0:T(1024)S(1)}, f32[2048]{0:T(1024)}, u32[]{:S(2)}) copy-start(f32[2048]{0:T(1024)} %param.23) | copy-start | bytes 24580
  473.7 14.2 %copy-start.8 = (f32[16]{0:T(128)S(1)}, f32[16]{0:T(128)}, u32[]{:S(2)}) copy-start(f32[16]{0:T(128)} %dynamic_slice.6.part_x) | copy-start | bytes 196
  487.9 11.6 %copy-start.1 = (f32[512]{0:T(512)S(1)}, f32[512]{0:T(512)}, u32[]{:S(2)}) copy-start(f32[512]{0:T(512)} %param.22) | copy-start | bytes 6148
